TPU v7x, 32 devices: a whole 2x2x4 slice. The times are simulated.
32 devices in a mesh: grp: 4 (over z), seq: 8 (over y, x, core).
Axes of the slice: x: 2, y: 2, z: 4, core: 2. Of those that a mesh axis runs over, the one named last changes fastest.
Arguments:
- hist_keys: bfloat16 [4, 1024, 1024], P('grp', 'seq'), may hold values from -4 to 4
- hist_values: bfloat16 [4, 1024, 1024], P('grp', 'seq'), may hold values from -6 to 6
- latent_queries: bfloat16 [4, 64, 1024], P('grp', 'seq'), may hold values from -48 to 48
- latent_pos: int32 [4, 64], P('grp'), may hold values from 128 to 1023
- targets: int32 [4, 64], P('grp', 'seq'), may hold values from 0 to 127
- out_proj: bfloat16 [1024, 2048], P('seq'), may hold values from -0.1875 to 0.1875
- norm_gain: float32 [2048], replicated, may hold values from 0.1 to 1.9
- unembed: bfloat16 [2048, 128], replicated, may hold values from -0.125 to 0.125
Outputs:
- loss: float32 [4], P('grp')
- grad_queries: bfloat16 [4, 64, 1024], P('grp', 'seq')
- grad_keys: bfloat16 [4, 1024, 1024], P('grp', 'seq')
- grad_values: bfloat16 [4, 1024, 1024], P('grp', 'seq')
- proj_update: float32 [1024, 2048], P('seq')
All inputs are finite; a program needn't handle non-finite values.
Results may differ from a plain program's by a relative error of at most 0.03.
Values may be sent and summed in bfloat16 or wider, within the bound.
No kernel may reach another device: no remote copies, remote signals or barrier semaphores. Data moves between devices by JAX's collectives and lax.ppermute only.
A program may use at most 64 MiB of HBM per device.

v0:
```python
import jax
import jax.numpy as jnp
from jax import lax
from jax.sharding import PartitionSpec as P

D = 2048
HD = 128
epsilon = 1e-06
loss_factor = 64.0


def joined(part, axis, combine):
    gathered = jax.tree.map(lambda a: lax.all_gather(a, axis), part)

    def take(source):
        return jax.tree.map(lambda a: lax.dynamic_index_in_dim(a, source, 0, False), gathered)

    return lax.fori_loop(
        1, lax.axis_size(axis), lambda source, state: combine(state, take(source)), take(0)
    )


def repeat_heads(stat):
    return jnp.repeat(stat, HD, axis=-1)


def combine(earlier, later):
    best = jnp.maximum(earlier[0], later[0])
    factor_one = jnp.exp(earlier[0] - best)
    factor_two = jnp.exp(later[0] - best)
    denom = earlier[1] * factor_one + later[1] * factor_two
    summed = earlier[2] * repeat_heads(factor_one) + later[2] * repeat_heads(factor_two)
    return (best, denom, summed)


def body(hist_keys, hist_values, latent_queries, latent_pos, targets, out_proj, norm_gain, unembed):
    softmax_scale = HD ** (-0.5)
    seq_keys = hist_keys[0]
    seq_values = hist_values[0]
    position = lax.axis_index("seq")
    tok_rows = seq_keys.shape[0]
    channels = seq_keys.shape[1]
    head_count = channels // HD
    own_rows = latent_queries.shape[1]
    queries = lax.all_gather(latent_queries[0], "seq", axis=0, tiled=True)
    latents = queries.shape[0]
    query_heads = queries.reshape(latents, head_count, HD)
    key_heads = seq_keys.reshape(tok_rows, head_count, HD)
    value_heads = seq_values.reshape(tok_rows, head_count, HD)
    places = position * tok_rows + jnp.arange(tok_rows, dtype=jnp.int32)
    visible = (places[None, :] <= latent_pos[0][:, None])[None]
    scores = (
        jnp.einsum("ihd,jhd->hij", query_heads, key_heads, preferred_element_type=jnp.float32)
        * softmax_scale
    )
    largest = jnp.max(jnp.where(visible, scores, -1e30), axis=-1)
    weights = jnp.where(visible, jnp.exp(scores - largest[..., None]), 0.0)
    summed = jnp.sum(weights, axis=-1)
    partial_out = jnp.einsum(
        "hij,jhd->ihd",
        weights.astype(jnp.bfloat16),
        value_heads,
        preferred_element_type=jnp.float32,
    ).reshape(latents, channels)
    best, denom, combined = joined((largest.T, summed.T, partial_out), "seq", combine)
    attn_all = (combined / repeat_heads(denom)).astype(jnp.bfloat16)
    log_norm = best + jnp.log(denom)
    slab = out_proj.shape[0]
    attn_cols = lax.dynamic_slice_in_dim(attn_all, position * slab, slab, 1)
    proj_columns = lax.all_to_all(out_proj, "seq", split_axis=1, concat_axis=0, tiled=True)
    column_block = jnp.dot(attn_all, proj_columns, preferred_element_type=jnp.float32)
    hidden = lax.all_to_all(column_block, "seq", split_axis=0, concat_axis=1, tiled=True)
    inverse = lax.rsqrt(jnp.mean(hidden * hidden, axis=-1, keepdims=True) + epsilon)
    normed = (hidden * inverse * norm_gain).astype(jnp.bfloat16)
    logits = jnp.dot(normed, unembed, preferred_element_type=jnp.float32)
    log_total = jax.nn.logsumexp(logits, axis=-1, keepdims=True)
    onehot = (jnp.arange(logits.shape[1], dtype=jnp.int32)[None, :] == targets[0][:, None]).astype(
        jnp.float32
    )
    local_loss = jnp.sum(log_total[:, 0] - jnp.sum(logits * onehot, axis=-1))
    grad_logits = (loss_factor * (jnp.exp(logits - log_total) - onehot)).astype(jnp.bfloat16)
    grad_normed = lax.dot_general(
        grad_logits, unembed, (((1,), (1,)), ((), ())), preferred_element_type=jnp.float32
    )
    scaled = norm_gain * grad_normed
    grad_hidden = (
        inverse * scaled - hidden * inverse**3 * jnp.mean(hidden * scaled, axis=-1, keepdims=True)
    ).astype(jnp.bfloat16)
    grad_all = lax.all_gather(grad_hidden, "seq", axis=0, tiled=True)
    weight_part = lax.dot_general(
        attn_cols, grad_all, (((0,), (0,)), ((), ())), preferred_element_type=jnp.float32
    )
    grad_cols = lax.dot_general(
        grad_all, out_proj, (((1,), (1,)), ((), ())), preferred_element_type=jnp.float32
    ).astype(jnp.bfloat16)
    grad_attn = lax.all_gather(grad_cols, "seq", axis=1, tiled=True)
    grad_heads = grad_attn.reshape(latents, head_count, HD)
    product = grad_attn.astype(jnp.float32) * attn_all.astype(jnp.float32)
    delta = jnp.sum(product.reshape(latents, head_count, HD), axis=-1)
    probs = jnp.where(visible, jnp.exp(scores - log_norm.T[..., None]), 0.0)
    grad_probs = jnp.einsum(
        "ihd,jhd->hij", grad_heads, value_heads, preferred_element_type=jnp.float32
    )
    grad_scores = (probs * (grad_probs - delta.T[..., None])).astype(jnp.bfloat16)
    grad_values = (
        jnp.einsum(
            "hij,ihd->jhd",
            probs.astype(jnp.bfloat16),
            grad_heads,
            preferred_element_type=jnp.float32,
        )
        .reshape(tok_rows, channels)
        .astype(jnp.bfloat16)
    )
    grad_keys = (
        (
            jnp.einsum("hij,ihd->jhd", grad_scores, query_heads, preferred_element_type=jnp.float32)
            * softmax_scale
        )
        .reshape(tok_rows, channels)
        .astype(jnp.bfloat16)
    )
    terms = jnp.einsum("hij,jhd->ihd", grad_scores, key_heads, preferred_element_type=jnp.float32)
    grad_queries = lax.psum_scatter(
        (terms.reshape(lax.axis_size("seq") * own_rows, channels) * softmax_scale).astype(
            jnp.bfloat16
        ),
        "seq",
        scatter_dimension=0,
        tiled=True,
    )
    entries = channels * D
    weight_sum = lax.psum(weight_part.astype(jnp.bfloat16), "grp").astype(jnp.float32)
    loss_sum, square_sum = lax.psum((local_loss, jnp.sum(weight_sum * weight_sum)), "seq")
    proj_update = weight_sum * lax.rsqrt(square_sum / entries + epsilon)
    return (
        loss_sum.reshape(1),
        grad_queries[None],
        grad_keys[None],
        grad_values[None],
        proj_update,
    )


def solution(mesh):
    placed = (
        P("grp", "seq", None),
        P("grp", "seq", None),
        P("grp", "seq", None),
        P("grp", None),
        P("grp", "seq"),
        P("seq", None),
        P(),
        P(),
    )
    return jax.shard_map(
        body,
        mesh=mesh,
        in_specs=placed,
        out_specs=(
            P("grp"),
            P("grp", "seq", None),
            P("grp", "seq", None),
            P("grp", "seq", None),
            P("seq", None),
        ),
        check_vma=False,
    )
```

profile of v0, /device:TPU:0, one launch (start us, length us, event | category | flops | bytes accessed | tf_op | source)
XLA Modules:
  0.0 178.7 jit_solution(14543328704458842982)
XLA Ops:
  7.2 11.0 %all-gather = bf16[1,64,1024]{2,1,0:T(8,128)(2,1)S(1)} all-gather(bf16[1,8,1024]{2,1,0:T(8,128)(2,1)} %param.12), channel_id=2, replica_groups=mesh['grp'=4,'seq'=8] {'seq'}, dimensions={1}, use_global_device_ids=true | all-gather | bytes 147456 | tf_op jit(solution)/shard_map/all_gather | solution.py:45
  18.3 1.0 copy.64
  19.3 1.0 copy.65
  20.3 0.7 broadcast_compare_fusion
  21.1 0.4 select_reduce_fusion
  21.4 0.3 convolution_bitcast_fusion
  21.7 0.2 copy.46
  21.9 0.7 all_gather_reshape.3
  22.6 0.8 copy.97
  23.5 3.5 %all-to-all-start = ((bf16[128,8,256]{2,0,1:T(8,128)(2,1)}), bf16[128,8,256]{2,0,1:T(8,128)(2,1)S(1)}, u32[]{:S(2)}, u32[]{:S(2)}) async-start(bf16[128,8,256]{2,0,1:T(8,128)(2,1)} %bitcast.109), calls=%async_computation | async-start | bytes 1048576 | tf_op jit(solution)/shard_map/all_to_all | solution.py:70
  27.0 0.3 fusion.15
  27.3 14.3 %all-gather.4 = f32[8,64,8]{1,2,0:T(8,128)S(1)} all-gather(f32[1,64,8]{1,2,0:T(8,128)S(1)} %bitcast.146), channel_id=4, replica_groups=mesh['grp'=4,'seq'=8] {'seq'}, dimensions={0}, use_global_device_ids=true | all-gather | bytes 18432 | tf_op jit(solution)/shard_map/all_gather | solution.py:13
  41.5 9.5 %all-gather.3 = f32[8,64,8]{1,2,0:T(8,128)S(1)} all-gather(f32[1,64,8]{1,2,0:T(8,128)S(1)} %bitcast.145), channel_id=3, replica_groups=mesh['grp'=4,'seq'=8] {'seq'}, dimensions={0}, use_global_device_ids=true | all-gather | bytes 18432 | tf_op jit(solution)/shard_map/all_gather | solution.py:13
  51.0 2.8 %all-gather.7.cloned.1.call-done = f32[8,64,1024]{2,1,0:T(8,128)} async-done(((f32[1,64,1024]{2,1,0:T(8,128)}), f32[8,64,1024]{2,1,0:T(8,128)}) %all-gather.7.cloned.1.call-update) | async-done | bytes 2097168 | tf_op jit(solution)/shard_map/all_gather | solution.py:13
  53.8 1.0 slice_bitcast_fusion
  54.7 11.5 %while.19 = (s32[]{:T(128)}, f32[64,8]{0,1:T(8,128)S(1)}, f32[64,8]{0,1:T(8,128)S(1)}, f32[64,1024]{1,0:T(8,128)S(1)}, f32[8,64,8]{1,2,0:T(8,128)S(1)}, /*index=...) while((s32[]{:T(128)}, f32[64,8]{0,1:T(8,128)S(1)}, ...), condition=%wide.region_3.4_spmd, body=%wide.region_2.3_spmd.sunk | while | flops 199685 | bytes 1863823 | solution.py:18
  55.2 1.2 fusion.60
  56.9 1.2 fusion.60
  58.5 1.2 fusion.60
  60.1 1.2 fusion.60
  61.8 1.2 fusion.60
  63.4 1.2 fusion.60
  65.1 1.2 fusion.60
  66.6 0.8 fusion.21
  67.4 3.4 %all-to-all-start.1 = ((f32[8,8,256]{2,1,0:T(8,128)}), f32[8,8,256]{2,1,0:T(8,128)S(1)}, u32[]{:S(2)}, u32[]{:S(2)}) async-start(f32[8,8,256]{2,1,0:T(8,128)} %fusion.21), calls=%async_computation.1 | async-start | bytes 131072 | tf_op jit(solution)/shard_map/all_to_all | solution.py:72
  70.8 4.9 %all-to-all-done.1 = f32[8,8,256]{2,1,0:T(8,128)S(1)} async-done(((f32[8,8,256]{2,1,0:T(8,128)}), f32[8,8,256]{2,1,0:T(8,128)S(1)}, u32[]{:S(2)}, u32[]{:S(2)}) %all-to-all-start.1) | async-done | bytes 65568 | tf_op jit(solution)/shard_map/all_to_all | solution.py:72
  75.7 0.1 fusion.33
  75.9 0.3 fusion.46
  76.3 0.2 select_reduce_fusion.1
  76.5 0.6 subtract_reduce_fusion
  77.1 0.4 multiply_reduce_fusion
  77.6 8.3 %all_gather.30 = bf16[64,2048]{1,0:T(8,128)(2,1)S(1)} all-gather(bf16[8,2048]{1,0:T(8,128)(2,1)S(1)} %subtract_convert_fusion), channel_id=1, replica_groups=mesh['grp'=4,'seq'=8] {'seq'}, dimensions={0}, use_global_device_ids=true | all-gather | bytes 294912 | tf_op jit(solution)/shard_map/all_gather | solution.py:89
  85.9 0.3 convolution_convert_fusion.2
  86.3 9.0 %all_gather.31 = bf16[64,1024]{1,0:T(8,128)(2,1)S(1)} all-gather(bf16[64,128]{1,0:T(8,128)(2,1)S(1)} %convolution_convert_fusion.2), channel_id=1, replica_groups=mesh['grp'=4,'seq'=8] {'seq'}, dimensions={1}, use_global_device_ids=true | all-gather | bytes 147456 | tf_op jit(solution)/shard_map/all_gather | solution.py:96
  95.3 1.1 convolution_convert_fusion
  96.6 0.1 reduce_sum.78
  96.8 0.3 fusion.5
  97.1 0.3 fusion.3
  97.4 0.8 copy.56
  98.2 0.2 fusion.7
  98.4 0.7 copy.98
  99.1 0.4 convolution_convert_fusion.1
  99.5 0.8 copy.57
  100.4 34.9 %all-reduce.3.cloned.1.call-done = bf16[128,2048]{1,0:T(8,128)(2,1)} async-done(((bf16[128,2048]{1,0:T(8,128)(2,1)}), bf16[128,2048]{1,0:T(8,128)(2,1)}) %all-reduce.3.cloned.1.call-update) | async-done | bytes 524304 | tf_op jit(solution)/shard_map/psum | solution.py:133
  135.2 1.9 %fusion.8 = f32[]{:T(128)} fusion(bf16[128,2048]{1,0:T(8,128)(2,1)} %all-reduce.3.cloned.1.call-done), kind=kLoop, calls=%fused_computation.25 | loop fusion | flops 786431 | bytes 524292 | tf_op jit(solution)/shard_map/reduce_sum | solution.py:134
  137.1 13.3 %all-reduce = (f32[1]{0:T(128)}, f32[]{:T(128)}) all-reduce(f32[1]{0:T(128)} %bitcast.19, f32[]{:T(128)} %fusion.8), channel_id=1, replica_groups=mesh['grp'=4,'seq'=8] {'seq'}, use_global_device_ids=true, to_apply=%region_9.10 | all-reduce | flops 2 | bytes 16 | tf_op jit(solution)/shard_map/psum | solution.py:134
  151.2 2.1 %convert_multiply_fusion = f32[128,2048]{1,0:T(8,128)} fusion(bf16[128,2048]{1,0:T(8,128)(2,1)} %all-reduce.3.cloned.1.call-done, f32[]{:T(128)S(6)} %rsqrt.15), kind=kLoop, calls=%fused_computation.11 | loop fusion | flops 524288 | bytes 1572868 | tf_op jit(solution)/shard_map/mul | solution.py:135
  153.3 18.9 %reduce-scatter.2.cloned.1.call-done = bf16[8,1024]{1,0:T(8,128)(2,1)} async-done(((bf16[64,1024]{1,0:T(8,128)(2,1)}), bf16[8,1024]{1,0:T(8,128)(2,1)}) %reduce-scatter.2.cloned.1.call-update) | async-done | bytes 16400 | tf_op jit(solution)/shard_map/reduce_scatter | solution.py:124
  (65 shorter events, 3.8 us)
Async XLA Ops:
  7.2 68.7 %copy-start = (bf16[2048,128]{1,0:T(8,128)(2,1)S(1)}, bf16[2048,128]{1,0:T(8,128)(2,1)}, u32[]{:S(2)}) copy-start(bf16[2048,128]{1,0:T(8,128)(2,1)} %param.17) | copy-start | bytes 1572868
  7.2 46.6 %all-gather.7.cloned.1.call-start = ((), (), s32[]{:S(2)}) async-start(), calls=%async_computation.3 | async-start | bytes 2359296 | tf_op jit(solution)/shard_map/all_gather | solution.py:13
  18.2 4.4 %copy-start.1 = (bf16[128,2048]{1,0:T(8,128)(2,1)S(1)}, bf16[128,2048]{1,0:T(8,128)(2,1)}, u32[]{:S(2)}) copy-start(bf16[128,2048]{1,0:T(8,128)(2,1)} %param.15) | copy-start | bytes 1572868
  23.5 43.1 %all-to-all-start = ((bf16[128,8,256]{2,0,1:T(8,128)(2,1)}), bf16[128,8,256]{2,0,1:T(8,128)(2,1)S(1)}, u32[]{:S(2)}, u32[]{:S(2)}) async-start(bf16[128,8,256]{2,0,1:T(8,128)(2,1)} %bitcast.109), calls=%async_computation | async-start | bytes 1048576 | tf_op jit(solution)/shard_map/all_to_all | solution.py:70
  54.7 21.2 %copy-start.2 = (f32[2048]{0:T(1024)S(1)}, f32[2048]{0:T(1024)}, u32[]{:S(2)}) copy-start(f32[2048]{0:T(1024)} %param.16) | copy-start | bytes 24580
  66.3 10.0 %copy-start.3 = (s32[1,8]{1,0:T(1,128)S(1)}, s32[1,8]{1,0:T(1,128)}, u32[]{:S(2)}) copy-start(s32[1,8]{1,0:T(1,128)} %param.14) | copy-start | bytes 100
  67.4 8.3 %all-to-all-start.1 = ((f32[8,8,256]{2,1,0:T(8,128)}), f32[8,8,256]{2,1,0:T(8,128)S(1)}, u32[]{:S(2)}, u32[]{:S(2)}) async-start(f32[8,8,256]{2,1,0:T(8,128)} %fusion.21), calls=%async_computation.1 | async-start | bytes 131072 | tf_op jit(solution)/shard_map/all_to_all | solution.py:72
  70.8 64.4 %all-reduce.3.cloned.1.call-start = ((), (), s32[]{:S(2)}) async-start(), calls=%async_computation.5 | async-start | bytes 1048576 | tf_op jit(solution)/shard_map/psum | solution.py:133
  96.4 75.8 %reduce-scatter.2.cloned.1.call-start = ((), (), s32[]{:S(2)}) async-start(), calls=%async_computation.4 | async-start | bytes 147456 | tf_op jit(solution)/shard_map/reduce_scatter | solution.py:124
Sparse Core Ops, SparseCore 0:
  22.8 30.9 all-gather.6
  96.5 38.6 all-reduce.2
  138.8 33.3 reduce-scatter.1
where the time goes:
time: 180 us; the launch traced here: 179 us
  blocking collectives  65.4 us (36%)
  waiting for transfers between devices  61.5 us (34%)
  other arithmetic  14.7 us (8%)
  between operations  14.7 us (8%)
  local copies, waits for them, and re-layouts  10.4 us (6%)
  starting transfers between devices  6.97 us (4%)
  matrix products  4.78 us (3%)
    psum x1, waiting for transfers between devices, body(): lax.psum(weight_part.astype(jnp.bfloat16), 'grp').astype(jnp.float32)  34.9 us
    all_gather x2, blocking collectives, joined(): gathered = jax.tree.map(lambda a: lax.all_gather(a, axis), part)  23.7 us
    reduce_scatter x1, waiting for transfers between devices, body(): lax.psum_scatter((terms.reshape(lax.axis_size('seq') * own_rows, channels...  18.9 us
    psum x1, blocking collectives, body(): lax.psum((local_loss, jnp.sum(weight_sum * weight_sum)), 'seq')  13.3 us
    all_gather x1, blocking collectives, body(): queries = lax.all_gather(latent_queries[0], 'seq', axis=0, tiled=True)  11 us
    all_gather x1, blocking collectives, body(): grad_attn = lax.all_gather(grad_cols, 'seq', axis=1, tiled=True)  9.03 us
    all_gather x1, blocking collectives, body(): grad_all = lax.all_gather(grad_hidden, 'seq', axis=0, tiled=True)  8.34 us
    add x7, other arithmetic, combine(): earlier[2] * repeat_heads(factor_one) + later[2] * repeat_heads(factor_two)  8.21 us
  transfers between devices with their start and end apart: 5, of which 4 were waited for; matrix products, arithmetic and copies ran while one was open for 12% of the time, Pallas kernels for 0%

commit v1 on v0

--- a/solution.py
+++ b/solution.py
@@ -130,7 +130,9 @@
         tiled=True,
     )
     entries = channels * D
-    weight_sum = lax.psum(weight_part.astype(jnp.bfloat16), "grp").astype(jnp.float32)
+    weight_sum = jnp.sum(lax.all_gather(weight_part.astype(jnp.bfloat16), "grp"), axis=0).astype(
+        jnp.float32
+    )
     loss_sum, square_sum = lax.psum((local_loss, jnp.sum(weight_sum * weight_sum)), "seq")
     proj_update = weight_sum * lax.rsqrt(square_sum / entries + epsilon)
     return (

time: 180 us -> 176 us (0.978)
  waiting for transfers between devices: 61.5 us -> 57.5 us
    psum x1 -> x0, waiting for transfers between devices: 34.9 us -> none  [body(): lax.psum(weight_part.astype(jnp.bfloat16), 'grp').astype(jnp.float32)]
    all_gather x0 -> x1, waiting for transfers between devices: none -> 32.5 us  [body(): lax.all_gather(weight_part.astype(jnp.bfloat16), 'grp')]
    reduce_sum x0 -> x1, other arithmetic: none -> 2.02 us  [body(): jnp.sum(lax.all_gather(weight_part.astype(jnp.bfloat16), 'grp'), axis=0)]
where the time goes in v1:
time: 176 us; the launch traced here: 175 us
  blocking collectives  66.2 us (38%)
  waiting for transfers between devices  57.5 us (33%)
  between operations  14.7 us (8%)
  other arithmetic  14.6 us (8%)
  local copies, waits for them, and re-layouts  10.4 us (6%)
  starting transfers between devices  6.97 us (4%)
  matrix products  4.77 us (3%)
    all_gather x1, waiting for transfers between devices, body(): lax.all_gather(weight_part.astype(jnp.bfloat16), 'grp')  32.5 us
    all_gather x2, blocking collectives, joined(): gathered = jax.tree.map(lambda a: lax.all_gather(a, axis), part)  23.7 us
    reduce_scatter x1, waiting for transfers between devices, body(): lax.psum_scatter((terms.reshape(lax.axis_size('seq') * own_rows, channels...  17.3 us
    psum x1, blocking collectives, body(): lax.psum((local_loss, jnp.sum(weight_sum * weight_sum)), 'seq')  14.1 us
    all_gather x1, blocking collectives, body(): queries = lax.all_gather(latent_queries[0], 'seq', axis=0, tiled=True)  11 us
    all_gather x1, blocking collectives, body(): grad_attn = lax.all_gather(grad_cols, 'seq', axis=1, tiled=True)  9.03 us
    all_gather x1, blocking collectives, body(): grad_all = lax.all_gather(grad_hidden, 'seq', axis=0, tiled=True)  8.34 us
    add x7, other arithmetic, combine(): earlier[2] * repeat_heads(factor_one) + later[2] * repeat_heads(factor_two)  8.21 us
  transfers between devices with their start and end apart: 5, of which 4 were waited for; matrix products, arithmetic and copies ran while one was open for 12% of the time, Pallas kernels for 0%

profile of v1, /device:TPU:0, one launch (start us, length us, event | category | flops | bytes accessed | tf_op | source)
XLA Modules:
  0.0 175.4 jit_solution(5640138102276530314)
XLA Ops:
  7.2 11.0 %all-gather = bf16[1,64,1024]{2,1,0:T(8,128)(2,1)S(1)} all-gather(bf16[1,8,1024]{2,1,0:T(8,128)(2,1)} %param.12), channel_id=2, replica_groups=mesh['grp'=4,'seq'=8] {'seq'}, dimensions={1}, use_global_device_ids=true | all-gather | bytes 147456 | tf_op jit(solution)/shard_map/all_gather | solution.py:45
  18.3 1.0 copy.64
  19.3 1.0 copy.65
  20.3 0.7 broadcast_compare_fusion
  21.1 0.4 select_reduce_fusion
  21.4 0.3 convolution_bitcast_fusion
  21.7 0.2 copy.46
  21.9 0.7 all_gather_reshape.3
  22.6 0.8 copy.97
  23.5 3.5 %all-to-all-start = ((bf16[128,8,256]{2,0,1:T(8,128)(2,1)}), bf16[128,8,256]{2,0,1:T(8,128)(2,1)S(1)}, u32[]{:S(2)}, u32[]{:S(2)}) async-start(bf16[128,8,256]{2,0,1:T(8,128)(2,1)} %bitcast.110), calls=%async_computation | async-start | bytes 1048576 | tf_op jit(solution)/shard_map/all_to_all | solution.py:70
  27.0 0.3 fusion.15
  27.3 14.3 %all-gather.5 = f32[8,64,8]{1,2,0:T(8,128)S(1)} all-gather(f32[1,64,8]{1,2,0:T(8,128)S(1)} %bitcast.148), channel_id=4, replica_groups=mesh['grp'=4,'seq'=8] {'seq'}, dimensions={0}, use_global_device_ids=true | all-gather | bytes 18432 | tf_op jit(solution)/shard_map/all_gather | solution.py:13
  41.5 9.5 %all-gather.4 = f32[8,64,8]{1,2,0:T(8,128)S(1)} all-gather(f32[1,64,8]{1,2,0:T(8,128)S(1)} %bitcast.147), channel_id=3, replica_groups=mesh['grp'=4,'seq'=8] {'seq'}, dimensions={0}, use_global_device_ids=true | all-gather | bytes 18432 | tf_op jit(solution)/shard_map/all_gather | solution.py:13
  51.0 2.8 %all-gather.9.cloned.1.call-done = f32[8,64,1024]{2,1,0:T(8,128)} async-done(((f32[1,64,1024]{2,1,0:T(8,128)}), f32[8,64,1024]{2,1,0:T(8,128)}) %all-gather.9.cloned.1.call-update) | async-done | bytes 2097168 | tf_op jit(solution)/shard_map/all_gather | solution.py:13
  53.8 1.0 slice_bitcast_fusion
  54.7 11.5 %while.19 = (s32[]{:T(128)}, f32[64,8]{0,1:T(8,128)S(1)}, f32[64,8]{0,1:T(8,128)S(1)}, f32[64,1024]{1,0:T(8,128)S(1)}, f32[8,64,8]{1,2,0:T(8,128)S(1)}, /*index=...) while((s32[]{:T(128)}, f32[64,8]{0,1:T(8,128)S(1)}, ...), condition=%wide.region_3.4_spmd, body=%wide.region_2.3_spmd.sunk | while | flops 199685 | bytes 1863823 | solution.py:18
  55.2 1.2 fusion.60
  56.9 1.2 fusion.60
  58.5 1.2 fusion.60
  60.1 1.2 fusion.60
  61.8 1.2 fusion.60
  63.4 1.2 fusion.60
  65.1 1.2 fusion.60
  66.6 0.8 fusion.21
  67.4 3.4 %all-to-all-start.1 = ((f32[8,8,256]{2,1,0:T(8,128)}), f32[8,8,256]{2,1,0:T(8,128)S(1)}, u32[]{:S(2)}, u32[]{:S(2)}) async-start(f32[8,8,256]{2,1,0:T(8,128)} %fusion.21), calls=%async_computation.1 | async-start | bytes 131072 | tf_op jit(solution)/shard_map/all_to_all | solution.py:72
  70.8 4.9 %all-to-all-done.1 = f32[8,8,256]{2,1,0:T(8,128)S(1)} async-done(((f32[8,8,256]{2,1,0:T(8,128)}), f32[8,8,256]{2,1,0:T(8,128)S(1)}, u32[]{:S(2)}, u32[]{:S(2)}) %all-to-all-start.1) | async-done | bytes 65568 | tf_op jit(solution)/shard_map/all_to_all | solution.py:72
  75.9 0.3 fusion.46
  76.3 0.2 select_reduce_fusion.1
  76.5 0.6 subtract_reduce_fusion
  77.1 0.4 multiply_reduce_fusion
  77.6 8.3 %all_gather.36 = bf16[64,2048]{1,0:T(8,128)(2,1)S(1)} all-gather(bf16[8,2048]{1,0:T(8,128)(2,1)S(1)} %subtract_convert_fusion), channel_id=1, replica_groups=mesh['grp'=4,'seq'=8] {'seq'}, dimensions={0}, use_global_device_ids=true | all-gather | bytes 294912 | tf_op jit(solution)/shard_map/all_gather | solution.py:89
  85.9 1.1 convolution_convert_fusion
  87.1 0.3 convolution_convert_fusion.2
  87.4 9.0 %all_gather.37 = bf16[64,1024]{1,0:T(8,128)(2,1)S(1)} all-gather(bf16[64,128]{1,0:T(8,128)(2,1)S(1)} %convolution_convert_fusion.2), channel_id=1, replica_groups=mesh['grp'=4,'seq'=8] {'seq'}, dimensions={1}, use_global_device_ids=true | all-gather | bytes 147456 | tf_op jit(solution)/shard_map/all_gather | solution.py:96
  96.6 0.1 reduce_sum.90
  96.8 0.3 fusion.5
  97.1 0.3 fusion.3
  97.4 0.8 copy.56
  98.2 0.2 fusion.7
  98.4 0.7 copy.98
  99.1 0.4 convolution_convert_fusion.1
  99.5 0.8 copy.57
  100.4 32.5 %all-gather.11.cloned.1.call-done = bf16[512,2048]{1,0:T(8,128)(2,1)} async-done(((bf16[128,2048]{1,0:T(8,128)(2,1)}), bf16[512,2048]{1,0:T(8,128)(2,1)}) %all-gather.11.cloned.1.call-update) | async-done | bytes 2097168 | tf_op jit(solution)/shard_map/all_gather | solution.py:133
  132.9 2.0 %reduce_sum.91 = bf16[128,2048]{1,0:T(8,128)(2,1)S(1)} reduce(bf16[4,128,2048]{2,1,0:T(8,128)(2,1)} %bitcast.126, bf16[]{:T(256)} %constant.86.clone.1), dimensions={0}, to_apply=%region_13.14 | reduce | flops 786432 | bytes 2621442 | tf_op jit(solution)/shard_map/reduce_sum | solution.py:133
  134.9 0.9 fusion.8
  135.8 14.1 %all-reduce = (f32[1]{0:T(128)}, f32[]{:T(128)}) all-reduce(f32[1]{0:T(128)} %bitcast.19, f32[]{:T(128)} %fusion.8), channel_id=1, replica_groups=mesh['grp'=4,'seq'=8] {'seq'}, use_global_device_ids=true, to_apply=%region_9.10 | all-reduce | flops 2 | bytes 16 | tf_op jit(solution)/shard_map/psum | solution.py:136
  150.5 1.1 convert_multiply_fusion
  151.6 17.3 %reduce-scatter.2.cloned.1.call-done = bf16[8,1024]{1,0:T(8,128)(2,1)} async-done(((bf16[64,1024]{1,0:T(8,128)(2,1)}), bf16[8,1024]{1,0:T(8,128)(2,1)}) %reduce-scatter.2.cloned.1.call-update) | async-done | bytes 16400 | tf_op jit(solution)/shard_map/reduce_scatter | solution.py:124
  (66 shorter events, 3.9 us)
Async XLA Ops:
  7.2 68.7 %copy-start = (bf16[2048,128]{1,0:T(8,128)(2,1)S(1)}, bf16[2048,128]{1,0:T(8,128)(2,1)}, u32[]{:S(2)}) copy-start(bf16[2048,128]{1,0:T(8,128)(2,1)} %param.17) | copy-start | bytes 1572868
  7.2 46.6 %all-gather.9.cloned.1.call-start = ((), (), s32[]{:S(2)}) async-start(), calls=%async_computation.3 | async-start | bytes 2359296 | tf_op jit(solution)/shard_map/all_gather | solution.py:13
  18.2 4.4 %copy-start.1 = (bf16[128,2048]{1,0:T(8,128)(2,1)S(1)}, bf16[128,2048]{1,0:T(8,128)(2,1)}, u32[]{:S(2)}) copy-start(bf16[128,2048]{1,0:T(8,128)(2,1)} %param.15) | copy-start | bytes 1572868
  23.5 43.1 %all-to-all-start = ((bf16[128,8,256]{2,0,1:T(8,128)(2,1)}), bf16[128,8,256]{2,0,1:T(8,128)(2,1)S(1)}, u32[]{:S(2)}, u32[]{:S(2)}) async-start(bf16[128,8,256]{2,0,1:T(8,128)(2,1)} %bitcast.110), calls=%async_computation | async-start | bytes 1048576 | tf_op jit(solution)/shard_map/all_to_all | solution.py:70
  54.7 21.2 %copy-start.2 = (f32[2048]{0:T(1024)S(1)}, f32[2048]{0:T(1024)}, u32[]{:S(2)}) copy-start(f32[2048]{0:T(1024)} %param.16) | copy-start | bytes 24580
  66.3 10.0 %copy-start.3 = (s32[1,8]{1,0:T(1,128)S(1)}, s32[1,8]{1,0:T(1,128)}, u32[]{:S(2)}) copy-start(s32[1,8]{1,0:T(1,128)} %param.14) | copy-start | bytes 100
  67.4 8.3 %all-to-all-start.1 = ((f32[8,8,256]{2,1,0:T(8,128)}), f32[8,8,256]{2,1,0:T(8,128)S(1)}, u32[]{:S(2)}, u32[]{:S(2)}) async-start(f32[8,8,256]{2,1,0:T(8,128)} %fusion.21), calls=%async_computation.1 | async-start | bytes 131072 | tf_op jit(solution)/shard_map/all_to_all | solution.py:72
  70.8 62.1 %all-gather.11.cloned.1.call-start = ((), (), s32[]{:S(2)}) async-start(), calls=%async_computation.5 | async-start | bytes 2621440 | tf_op jit(solution)/shard_map/all_gather | solution.py:133
  87.1 81.8 %reduce-scatter.2.cloned.1.call-start = ((), (), s32[]{:S(2)}) async-start(), calls=%async_computation.4 | async-start | bytes 147456 | tf_op jit(solution)/shard_map/reduce_scatter | solution.py:124
Sparse Core Ops, SparseCore 0:
  22.8 30.9 all-gather.8
  87.2 45.6 all-gather.10
  136.5 32.3 reduce-scatter.1
